TPU v7x, 32 devices: a whole 2x2x4 slice. The times are simulated.
32 devices in a mesh: cuts: 4 (over z), row: 8 (over y, x, core).
Axes of the slice: x: 2, y: 2, z: 4, core: 2. Of those that a mesh axis runs over, the one named last changes fastest.
Arguments:
- eigvecs: float32 [16384, 2048], P('row', 'cuts'), may hold values from -1.2 to 1.2
- slice_counts: int32 [4], P('cuts'), may hold values from 256 to 512, as said below
- occ_index: int32 [2048], P('cuts'), may hold values from 0 to 63
- occ_levels: float32 [64], replicated, may hold values from 0 to 1
Outputs:
- slab: float32 [4096, 16384], P('cuts', 'row')
Inputs may be any that keep to these rules, and one draw needn't show every extreme that they name: `slice_counts`: some slice holds exactly 512 eigenvalues in every draw; the others at least half of that.
All inputs are finite; a program needn't handle non-finite values.
Results may differ from a plain program's by a relative error of at most 0.000062.
Values sent between devices are 32-bit elements; how exact they have to be, the bound alone decides.
No kernel may reach another device: no remote copies, remote signals or barrier semaphores. Data moves between devices by JAX's collectives and lax.ppermute only.
A program may use at most 128 MiB of HBM per device.

v0:
```python
import jax
import jax.numpy as jnp
from jax import lax
from jax.sharding import PartitionSpec as P

BLOCK = 1024
SLAB_SUB = 256
SLAB = 4096


def shards(eigvecs, slice_counts, occ_index, occ_levels):
    row_count = eigvecs.shape[0]
    slot_count = eigvecs.shape[1]
    level_ids = jnp.arange(occ_levels.shape[0], dtype=jnp.int32)
    one_hot = (occ_index[:, None] == level_ids[None, :]).astype(jnp.float32)
    values = jnp.dot(one_hot, occ_levels, precision=lax.Precision.HIGHEST)
    live = jnp.arange(slot_count, dtype=jnp.int32) < slice_counts[0]
    weights = jnp.where(live, values, jnp.float32(0.0))
    local_blocks = eigvecs.reshape(row_count // BLOCK, BLOCK, slot_count)[:, :SLAB_SUB, :]
    local_rows = local_blocks.reshape(-1, slot_count) * weights[None, :]
    cut_count = lax.axis_size("cuts")
    row_devices = lax.axis_size("row")
    owned = SLAB // cut_count
    strip = slot_count // row_devices
    spread = lax.all_to_all(local_rows.T, "row", split_axis=0, concat_axis=1, tiled=True)
    owners = lax.all_to_all(spread, "cuts", split_axis=1, concat_axis=0, tiled=True)
    panels = lax.all_gather(owners, "row", axis=0, tiled=True)
    panel = (
        panels.reshape(row_devices, cut_count, strip, owned)
        .transpose(1, 0, 2, 3)
        .reshape(cut_count * slot_count, owned)
    )
    return lax.dot_general(
        panel,
        lax.all_gather(eigvecs, "cuts", axis=1, tiled=True),
        (((0,), (1,)), ((), ())),
        precision=lax.Precision.HIGHEST,
        preferred_element_type=jnp.float32,
    )


def solution(mesh):
    return jax.shard_map(
        shards,
        mesh=mesh,
        in_specs=(P("row", "cuts"), P("cuts"), P("cuts"), P()),
        out_specs=P("cuts", "row"),
        check_vma=False,
    )
```

profile of v0, /device:TPU:0, one launch (start us, length us, event | category | flops | bytes accessed | tf_op | source)
XLA Modules:
  0.0 519.5 jit_solution(15764011367793498607)
XLA Ops:
  6.5 0.0 copy-start
  6.5 0.0 all-gather.3.cloned.1.call-start
  7.2 1.3 slice.4
  8.5 0.3 copy.14
  8.8 0.0 copy-done
  8.9 1.0 fusion
  9.9 0.2 broadcast_multiply_fusion
  10.0 20.3 %all_to_all.35 = f32[8,64,512]{2,1,0:T(8,128)S(1)} all-to-all(f32[8,64,512]{2,1,0:T(8,128)S(1)} %bitcast.24), channel_id=1, replica_groups=mesh['cuts'=4,'row'=8] {'row'}, dimensions={0} | all-to-all | bytes 2097152 | tf_op jit(solution)/shard_map/all_to_all | solution.py:25
  30.3 0.6 copy.10
  31.0 0.5 all_to_all.29
  31.5 0.6 copy.11
  32.1 29.9 %all_to_all.36 = f32[64,4,1024]{2,0,1:T(8,128)} all-to-all(f32[64,4,1024]{2,0,1:T(8,128)S(1)} %copy.11), channel_id=1, replica_groups=mesh['cuts'=4,'row'=8] {'cuts'}, dimensions={1} | all-to-all | bytes 2097152 | tf_op jit(solution)/shard_map/all_to_all | solution.py:26
  62.0 0.0 all-gather.3.cloned.1.call-update
  62.1 0.0 all-gather.5.cloned.1.call-start
  62.1 0.7 all-gather.5.cloned.1.call-update
  62.8 51.5 %all-gather.3.cloned.1.call-done = f32[2048,1024]{1,0:T(8,128)} async-done(((f32[256,1024]{1,0:T(8,128)}), f32[2048,1024]{1,0:T(8,128)}) %all-gather.3.cloned.1.call-update) | async-done | bytes 8388624 | tf_op jit(solution)/shard_map/all_gather | solution.py:27
  114.3 8.3 %copy.12 = f32[8,4,64,1024]{3,2,0,1:T(8,128)} copy(f32[8,4,64,1024]{3,2,1,0:T(8,128)} %bitcast.21) | data formatting | bytes 16777216 | tf_op jit(solution)/shard_map/reshape | solution.py:29
  122.6 280.1 %all-gather.5.cloned.1.call-done = f32[2048,2048]{1,0:T(8,128)} async-done(((f32[2048,512]{1,0:T(8,128)}), f32[2048,2048]{1,0:T(8,128)}) %all-gather.5.cloned.1.call-update) | async-done | bytes 16777232 | tf_op jit(solution)/shard_map/all_gather | solution.py:35
  402.7 110.0 %fusion.4 = f32[1024,2048]{1,0:T(8,128)} fusion(f32[2048,1024]{1,0:T(8,128)} %bitcast.22, f32[2048,2048]{1,0:T(8,128)} %all-gather.5.cloned.1.call-done), kind=kOutput, calls=%fused_computation.7 | convolution fusion | flops 51539607552 | bytes 33554432 | tf_op jit(solution)/shard_map/dot_general | solution.py:33
  (1 shorter events, 0.0 us)
Async XLA Ops:
  6.5 2.3 copy-start
  6.5 107.8 %all-gather.3.cloned.1.call-start = ((), (), s32[]{:S(2)}) async-start(), calls=%async_computation.2 | async-start | bytes 9437184 | tf_op jit(solution)/shard_map/all_gather | solution.py:27
  62.1 340.6 %all-gather.5.cloned.1.call-start = ((), (), s32[]{:S(2)}) async-start(), calls=%async_computation.3 | async-start | bytes 20971520 | tf_op jit(solution)/shard_map/all_gather | solution.py:35
Sparse Core Ops, SparseCore 0:
  62.2 52.0 all-gather.2
  115.9 286.7 all-gather.4
where the time goes:
time: 520 us; the launch traced here: 519 us
  waiting for transfers between devices  332 us (64%)
  matrix products  111 us (21%)
  blocking collectives  50.3 us (10%)
  between operations  14.1 us (3%)
  local copies, waits for them, and re-layouts  11.6 us (2%)
    all_gather x1, waiting for transfers between devices, shards(): lax.all_gather(eigvecs, 'cuts', axis=1, tiled=True)  280 us
    dot_general x1, matrix products, shards(): lax.dot_general(panel, lax.all_gather(eigvecs, 'cuts', axis=1, tiled=True...  110 us
    all_gather x1, waiting for transfers between devices, shards(): panels = lax.all_gather(owners, 'row', axis=0, tiled=True)  51.5 us
    all_to_all x1, blocking collectives, shards(): lax.all_to_all(spread, 'cuts', split_axis=1, concat_axis=0, tiled=True)  29.9 us
    all_to_all x1, blocking collectives, shards(): lax.all_to_all(local_rows.T, 'row', split_axis=0, concat_axis=1, tiled=True)  20.3 us
  transfers between devices with their start and end apart: 2, of which 2 were waited for; matrix products, arithmetic and copies ran while one was open for 2% of the time, Pallas kernels for 0%

commit v1 on v0

--- a/solution.py
+++ b/solution.py
@@ -24,7 +24,12 @@
     strip = slot_count // row_devices
     spread = lax.all_to_all(local_rows.T, "row", split_axis=0, concat_axis=1, tiled=True)
     owners = lax.all_to_all(spread, "cuts", split_axis=1, concat_axis=0, tiled=True)
-    panels = lax.all_gather(owners, "row", axis=0, tiled=True)
+    ring = [owners]
+    for hop in range(7):
+        ring.append(lax.ppermute(ring[-1], "row", [(dev, (dev + 1) % 8) for dev in range(8)]))
+    panels = jnp.roll(
+        jnp.concatenate(ring[::-1], axis=0), (lax.axis_index("row") + 1) * ring[0].shape[0], axis=0
+    )
     panel = (
         panels.reshape(row_devices, cut_count, strip, owned)
         .transpose(1, 0, 2, 3)

time: 520 us -> 438 us (0.84)
  waiting for transfers between devices: 332 us -> 197 us
  local copies, waits for them, and re-layouts: 11.6 us -> 41.1 us
  blocking collectives: 50.3 us -> 73.8 us
    all_gather x1, waiting for transfers between devices: 280 us -> 90.4 us  [shards(): lax.all_gather(eigvecs, 'cuts', axis=1, tiled=True)]
    ppermute x0 -> x7, waiting for transfers between devices: none -> 106 us  [shards(): lax.ppermute(ring[-1], 'row', [(dev, (dev + 1) % 8) for dev in range(8)])]
    all_gather x1 -> x0, waiting for transfers between devices: 51.5 us -> none  [shards(): panels = lax.all_gather(owners, 'row', axis=0, tiled=True)]
    unnamed x2 -> x31, local copies, waits for them, and re-layouts: 0.01 us -> 28.2 us
    all_to_all x1, blocking collectives: 29.9 us -> 53.5 us  [shards(): lax.all_to_all(spread, 'cuts', split_axis=1, concat_axis=0, tiled=True)]
    reshape x1 -> x0, local copies, waits for them, and re-layouts: 8.28 us -> none  [shards(): panels.reshape(row_devices, cut_count, strip, owned).transpose(1, 0, 2, 3)]
  transfers between devices with their start and end apart: 2 -> 8, of which waited for: 2 -> 8; matrix products, arithmetic and copies ran while one was open for 2% -> 9% of each run, Pallas kernels for 0% -> 0%
where the time goes in v1:
time: 438 us
  waiting for transfers between devices  197 us (45%)
  matrix products  111 us (25%)
  blocking collectives  73.8 us (17%)
  local copies, waits for them, and re-layouts  41.1 us (9%)
  between operations  14.1 us (3%)
    dot_general x1, matrix products, shards(): lax.dot_general(panel, lax.all_gather(eigvecs, 'cuts', axis=1, tiled=True...  110 us
    ppermute x7, waiting for transfers between devices, shards(): lax.ppermute(ring[-1], 'row', [(dev, (dev + 1) % 8) for dev in range(8)])  106 us
    all_gather x1, waiting for transfers between devices, shards(): lax.all_gather(eigvecs, 'cuts', axis=1, tiled=True)  90.4 us
    all_to_all x1, blocking collectives, shards(): lax.all_to_all(spread, 'cuts', split_axis=1, concat_axis=0, tiled=True)  53.5 us
    unnamed x31, local copies, waits for them, and re-layouts  28.2 us
    all_to_all x1, blocking collectives, shards(): lax.all_to_all(local_rows.T, 'row', split_axis=0, concat_axis=1, tiled=True)  20.3 us
  transfers between devices with their start and end apart: 8, of which 8 were waited for; matrix products, arithmetic and copies ran while one was open for 9% of the time, Pallas kernels for 0%

profile of v1, /device:TPU:0, one launch (start us, length us, event | category | flops | bytes accessed | tf_op | source)
XLA Modules:
  0.0 437.6 jit_solution(12167061029819645873)
XLA Ops:
  6.5 0.0 all-gather.2.cloned.1.call-start
  6.5 0.7 all-gather.2.cloned.1.call-update
  7.3 1.3 slice.4
  8.6 0.3 copy.17
  9.6 1.0 fusion
  10.6 0.1 broadcast_multiply_fusion
  10.7 20.3 %all_to_all.35 = f32[8,64,512]{2,1,0:T(8,128)S(1)} all-to-all(f32[8,64,512]{2,1,0:T(8,128)S(1)} %bitcast.27), channel_id=1, replica_groups=mesh['cuts'=4,'row'=8] {'row'}, dimensions={0} | all-to-all | bytes 2097152 | tf_op jit(solution)/shard_map/all_to_all | solution.py:25
  31.0 0.6 copy.13
  31.7 0.5 all_to_all.29
  32.2 0.6 copy.14
  32.8 53.5 %all_to_all.36 = f32[64,4,1024]{2,0,1:T(8,128)S(1)} all-to-all(f32[64,4,1024]{2,0,1:T(8,128)S(1)} %copy.14), channel_id=1, replica_groups=mesh['cuts'=4,'row'=8] {'cuts'}, dimensions={1} | all-to-all | bytes 2097152 | tf_op jit(solution)/shard_map/all_to_all | solution.py:26
  86.3 0.0 collective-permute-start
  86.3 15.1 %collective-permute-done = f32[256,1024]{1,0:T(8,128)S(1)} collective-permute-done((f32[256,1024]{1,0:T(8,128)S(1)}, f32[256,1024]{1,0:T(8,128)S(1)}, u32[]{:S(2)}, u32[]{:S(2)}) %collective-permute-start) | collective-permute-done | bytes 1048608 | tf_op jit(solution)/shard_map/ppermute | solution.py:29
  101.4 0.0 collective-permute-start.1
  101.4 15.1 %collective-permute-done.1 = f32[256,1024]{1,0:T(8,128)S(1)} collective-permute-done((f32[256,1024]{1,0:T(8,128)S(1)}, f32[256,1024]{1,0:T(8,128)S(1)}, u32[]{:S(2)}, u32[]{:S(2)}) %collective-permute-start.1) | collective-permute-done | bytes 1048608 | tf_op jit(solution)/shard_map/ppermute | solution.py:29
  116.6 0.0 collective-permute-start.2
  116.6 15.1 %collective-permute-done.2 = f32[256,1024]{1,0:T(8,128)S(1)} collective-permute-done((f32[256,1024]{1,0:T(8,128)S(1)}, f32[256,1024]{1,0:T(8,128)S(1)}, u32[]{:S(2)}, u32[]{:S(2)}) %collective-permute-start.2) | collective-permute-done | bytes 1048608 | tf_op jit(solution)/shard_map/ppermute | solution.py:29
  131.7 1.0 copy-done.2
  132.7 0.0 collective-permute-start.3
  132.7 15.1 %collective-permute-done.3 = f32[256,1024]{1,0:T(8,128)S(1)} collective-permute-done((f32[256,1024]{1,0:T(8,128)S(1)}, f32[256,1024]{1,0:T(8,128)S(1)}, u32[]{:S(2)}, u32[]{:S(2)}) %collective-permute-start.3) | collective-permute-done | bytes 1048608 | tf_op jit(solution)/shard_map/ppermute | solution.py:29
  147.8 1.0 copy-done.4
  148.8 0.0 collective-permute-start.4
  148.8 15.1 %collective-permute-done.4 = f32[256,1024]{1,0:T(8,128)S(1)} collective-permute-done((f32[256,1024]{1,0:T(8,128)S(1)}, f32[256,1024]{1,0:T(8,128)S(1)}, u32[]{:S(2)}, u32[]{:S(2)}) %collective-permute-start.4) | collective-permute-done | bytes 1048608 | tf_op jit(solution)/shard_map/ppermute | solution.py:29
  163.9 1.0 copy-done.6
  164.9 0.0 collective-permute-start.5
  164.9 15.2 %collective-permute-done.5 = f32[256,1024]{1,0:T(8,128)} collective-permute-done((f32[256,1024]{1,0:T(8,128)S(1)}, f32[256,1024]{1,0:T(8,128)}, u32[]{:S(2)}, u32[]{:S(2)}) %collective-permute-start.5) | collective-permute-done | bytes 1048608 | tf_op jit(solution)/shard_map/ppermute | solution.py:29
  180.1 0.0 collective-permute-start.6
  180.1 15.4 %collective-permute-done.6 = f32[256,1024]{1,0:T(8,128)} collective-permute-done((f32[256,1024]{1,0:T(8,128)}, f32[256,1024]{1,0:T(8,128)}, u32[]{:S(2)}, u32[]{:S(2)}) %collective-permute-start.6) | collective-permute-done | bytes 1048608 | tf_op jit(solution)/shard_map/ppermute | solution.py:29
  195.5 2.3 constant_dynamic-update-slice_fusion.15
  197.9 2.4 constant_dynamic-update-slice_fusion.14
  200.2 2.3 constant_dynamic-update-slice_fusion.13
  202.5 2.4 constant_dynamic-update-slice_fusion.12
  204.9 2.3 constant_dynamic-update-slice_fusion.11
  207.2 1.1 constant_dynamic-update-slice_fusion.10
  208.3 1.1 constant_dynamic-update-slice_fusion.9
  209.4 1.2 constant_dynamic-update-slice_fusion.8
  210.6 2.4 constant_dynamic-update-slice_fusion.7
  213.0 2.3 constant_dynamic-update-slice_fusion.6
  215.3 1.1 constant_dynamic-update-slice_fusion.5
  216.4 1.1 constant_dynamic-update-slice_fusion.4
  217.5 1.2 constant_dynamic-update-slice_fusion.3
  218.7 1.0 constant_dynamic-update-slice_fusion.2
  219.7 1.1 constant_dynamic-update-slice_fusion.1
  220.8 1.1 constant_dynamic-update-slice_fusion
  221.9 4.4 %constant_dynamic-slice_fusion = f32[2048,1024]{1,0:T(8,128)S(1)} fusion(f32[4096,1024]{1,0:T(8,128)} %constant_dynamic-update-slice_fusion, s32[]{:T(128)S(6)} %select_n.19), kind=kLoop, calls=%fused_computation.23 | loop fusion | bytes 16777220 | tf_op jit(solution)/shard_map/jit(_roll_dynamic)/dynamic_slice | solution.py:30
  226.3 4.1 copy.15
  230.4 90.4 %all-gather.2.cloned.1.call-done = f32[2048,2048]{1,0:T(8,128)} async-done(((f32[2048,512]{1,0:T(8,128)}), f32[2048,2048]{1,0:T(8,128)}) %all-gather.2.cloned.1.call-update) | async-done | bytes 16777232 | tf_op jit(solution)/shard_map/all_gather | solution.py:40
  320.8 110.0 %fusion.4 = f32[1024,2048]{1,0:T(8,128)} fusion(f32[2048,1024]{1,0:T(8,128)} %bitcast.25, f32[2048,2048]{1,0:T(8,128)} %all-gather.2.cloned.1.call-done), kind=kOutput, calls=%fused_computation.24 | convolution fusion | flops 51539607552 | bytes 33554432 | tf_op jit(solution)/shard_map/dot_general | solution.py:38
  (14 shorter events, 0.0 us)
Async XLA Ops:
  6.5 3.0 copy-start
  6.5 314.3 %all-gather.2.cloned.1.call-start = ((), (), s32[]{:S(2)}) async-start(), calls=%async_computation.2 | async-start | bytes 20971520 | tf_op jit(solution)/shard_map/all_gather | solution.py:40
  86.3 15.1 %collective-permute-start = (f32[256,1024]{1,0:T(8,128)S(1)}, f32[256,1024]{1,0:T(8,128)S(1)}, u32[]{:S(2)}, u32[]{:S(2)}) collective-permute-start(f32[256,1024]{1,0:T(8,128)S(1)} %bitcast.22), channel_id=1, source_target_pairs={{0,1},{1,2},{2,3},{3,4},{4,5},{5,6},{6,7},{7,0},{8,9},{9,10},{10,1... | collective-permute-start | bytes 3145736 | tf_op jit(solution)/shard_map/ppermute | solution.py:29
  101.4 15.1 %collective-permute-start.1 = (f32[256,1024]{1,0:T(8,128)S(1)}, f32[256,1024]{1,0:T(8,128)S(1)}, u32[]{:S(2)}, u32[]{:S(2)}) collective-permute-start(f32[256,1024]{1,0:T(8,128)S(1)} %collective-permute-done), channel_id=1, source_target_pairs={{0,1},{1,2},{2,3},{3,4},{4,5},{5,6},{6,7},{7,0},{8,9},{9,10},{10,1... | collective-permute-start | bytes 3145736 | tf_op jit(solution)/shard_map/ppermute | solution.py:29
  116.6 15.1 %collective-permute-start.2 = (f32[256,1024]{1,0:T(8,128)S(1)}, f32[256,1024]{1,0:T(8,128)S(1)}, u32[]{:S(2)}, u32[]{:S(2)}) collective-permute-start(f32[256,1024]{1,0:T(8,128)S(1)} %collective-permute-done.1), channel_id=1, source_target_pairs={{0,1},{1,2},{2,3},{3,4},{4,5},{5,6},{6,7},{7,0},{8,9},{9,10},{10,1... | collective-permute-start | bytes 3145736 | tf_op jit(solution)/shard_map/ppermute | solution.py:29
  131.7 1.0 copy-start.2
  132.7 15.1 %collective-permute-start.3 = (f32[256,1024]{1,0:T(8,128)S(1)}, f32[256,1024]{1,0:T(8,128)S(1)}, u32[]{:S(2)}, u32[]{:S(2)}) collective-permute-start(f32[256,1024]{1,0:T(8,128)S(1)} %collective-permute-done.2), channel_id=1, source_target_pairs={{0,1},{1,2},{2,3},{3,4},{4,5},{5,6},{6,7},{7,0},{8,9},{9,10},{10,1... | collective-permute-start | bytes 3145736 | tf_op jit(solution)/shard_map/ppermute | solution.py:29
  147.8 1.0 copy-start.4
  148.8 15.1 %collective-permute-start.4 = (f32[256,1024]{1,0:T(8,128)S(1)}, f32[256,1024]{1,0:T(8,128)S(1)}, u32[]{:S(2)}, u32[]{:S(2)}) collective-permute-start(f32[256,1024]{1,0:T(8,128)S(1)} %collective-permute-done.3), channel_id=1, source_target_pairs={{0,1},{1,2},{2,3},{3,4},{4,5},{5,6},{6,7},{7,0},{8,9},{9,10},{10,1... | collective-permute-start | bytes 3145736 | tf_op jit(solution)/shard_map/ppermute | solution.py:29
  163.9 1.0 copy-start.6
  164.9 15.2 %collective-permute-start.5 = (f32[256,1024]{1,0:T(8,128)S(1)}, f32[256,1024]{1,0:T(8,128)}, u32[]{:S(2)}, u32[]{:S(2)}) collective-permute-start(f32[256,1024]{1,0:T(8,128)S(1)} %collective-permute-done.4), channel_id=1, source_target_pairs={{0,1},{1,2},{2,3},{3,4},{4,5},{5,6},{6,7},{7,0},{8,9},{9,10},{10,1... | collective-permute-start | bytes 3145736 | tf_op jit(solution)/shard_map/ppermute | solution.py:29
  180.1 15.4 %collective-permute-start.6 = (f32[256,1024]{1,0:T(8,128)}, f32[256,1024]{1,0:T(8,128)}, u32[]{:S(2)}, u32[]{:S(2)}) collective-permute-start(f32[256,1024]{1,0:T(8,128)} %collective-permute-done.5), channel_id=1, source_target_pairs={{0,1},{1,2},{2,3},{3,4},{4,5},{5,6},{6,7},{7,0},{8,9},{9,10},{10,1... | collective-permute-start | bytes 3145736 | tf_op jit(solution)/shard_map/ppermute | solution.py:29
  180.1 35.2 %copy-start.7 = (f32[256,1024]{1,0:T(8,128)S(1)}, f32[256,1024]{1,0:T(8,128)}, u32[]{:S(2)}) copy-start(f32[256,1024]{1,0:T(8,128)} %copy-done.6) | copy-start | bytes 3145732
  180.1 36.3 %copy-start.5 = (f32[256,1024]{1,0:T(8,128)S(1)}, f32[256,1024]{1,0:T(8,128)}, u32[]{:S(2)}) copy-start(f32[256,1024]{1,0:T(8,128)} %copy-done.4) | copy-start | bytes 3145732
  180.1 37.4 %copy-start.3 = (f32[256,1024]{1,0:T(8,128)S(1)}, f32[256,1024]{1,0:T(8,128)}, u32[]{:S(2)}) copy-start(f32[256,1024]{1,0:T(8,128)} %copy-done.2) | copy-start | bytes 3145732
  320.8 110.0 %copy-start.1 = (f32[64]{0:T(128)S(1)}, f32[64]{0:T(128)}, u32[]{:S(2)}) copy-start(f32[64]{0:T(128)} %param.7) | copy-start | bytes 772
Sparse Core Ops, SparseCore 0:
  8.9 311.8 all-gather.1
